TPU v7x, 32 devices: a whole 2x2x4 slice. The times are simulated.
32 devices in a mesh: row: 4 (over y, core), col: 8 (over z, x).
Axes of the slice: x: 2, y: 2, z: 4, core: 2. Of those that a mesh axis runs over, the one named last changes fastest.
Arguments:
- right_side: float32 [5, 2, 64, 2048], P(None, None, None, 'row'), may hold values from -6 to 6
- panels: float32 [10, 2, 2048, 2048], P(None, None, 'row', 'col'), may hold values from -0.0625 to 0.0625
- diag_inverse: float32 [5, 2, 2048, 2048], P(None, None, 'row', 'col'), may hold values from -0.026516504 to 1.4
- parents: int32 [4, 2], replicated, may hold values from 0 to 1
- live_width: int32 [5, 2], replicated, may hold values from 1024 to 2048
- tile_pattern: int32 [10, 2, 16], replicated, may hold values 0 or 1
Outputs:
- interim: float32 [5, 2, 64, 2048], P(None, None, None, 'row')
- solution: float32 [5, 2, 64, 2048], P(None, None, None, 'row')
Inputs may be any that keep to these rules, and one draw needn't show every extreme that they name: parents[h, k] is the position on level h + 1 of the parent of supernode (h, k). The columns of supernode (h, k) from live_width[h, k] up to 2048 are padding. `tile_pattern`: 1 where the tile of 128 rows is present in the block.
All inputs are finite; a program needn't handle non-finite values.
Results may differ from a plain program's by a relative error of at most 0.0001.
Values sent between devices are 32-bit elements; how exact they have to be, the bound alone decides.
No kernel may reach another device: no remote copies, remote signals or barrier semaphores. Data moves between devices by JAX's collectives and lax.ppermute only.
A program may use at most 64 MiB of HBM per device.

v0:
```python
import jax
import jax.numpy as jnp
from jax import lax
from jax.sharding import PartitionSpec as P

TILE = 128
HIGHEST_PRECISION = lax.Precision.HIGHEST


def pair_index(lower, higher, depth_count):
    return lower * depth_count - lower * (lower + 1) // 2 + (higher - lower - 1)


def climb_maps(parents):
    depth_count = parents.shape[0] + 1
    width_count = parents.shape[1]
    positions = jnp.arange(width_count, dtype=jnp.int32)
    hop_maps = [
        (parents[height][:, None] == positions[None, :]).astype(jnp.float32)
        for height in range(depth_count - 1)
    ]
    climbs = {}
    for height in range(depth_count - 1):
        current = hop_maps[height]
        climbs[height, height + 1] = current
        for higher in range(height + 2, depth_count):
            current = jnp.dot(current, hop_maps[higher - 1], precision=HIGHEST_PRECISION)
            climbs[height, higher] = current
    return climbs


def per_device(right_side, panels, diag_inverse, parents, live_width, tile_pattern):
    levels = right_side.shape[0]
    per_level = right_side.shape[1]
    rhs_count = right_side.shape[2]
    row_span = right_side.shape[3]
    col_span = panels.shape[3]
    row_place = lax.axis_index("row")
    col_place = lax.axis_index("col")
    row_cells = row_place * row_span + jnp.arange(row_span, dtype=jnp.int32)
    col_cells = col_place * col_span + jnp.arange(col_span, dtype=jnp.int32)
    row_live = (row_cells[None, None, :] < live_width[:, :, None]).astype(jnp.float32)
    col_live = (col_cells[None, None, :] < live_width[:, :, None]).astype(jnp.float32)
    tile_count = row_span // TILE
    local_tiles = lax.dynamic_slice_in_dim(tile_pattern, row_place * tile_count, tile_count, 2)
    row_keep = jnp.repeat(local_tiles.astype(jnp.float32), TILE, axis=2)
    climbs = climb_maps(parents)

    def forward_turn(values):
        full_vector = lax.all_gather(values, "row", axis=2, tiled=True)
        return lax.dynamic_slice_in_dim(full_vector, col_place * col_span, col_span, 2)

    def backward_turn(values):
        full_vector = lax.all_gather(values, "col", axis=2, tiled=True)
        return lax.dynamic_slice_in_dim(full_vector, row_place * row_span, row_span, 2)

    pending = [jnp.zeros((per_level, rhs_count, row_span), jnp.float32) for height in range(levels)]
    interim = []
    for height in range(levels):
        if height > 0:
            summed = lax.psum(pending[height], "col")
            residual = right_side[height] - summed
        else:
            residual = right_side[height]
        turned = forward_turn(residual) * col_live[height][:, None, :]
        partial_solve = jnp.einsum(
            "kab,kjb->kja", diag_inverse[height], turned, precision=HIGHEST_PRECISION
        )
        solved = lax.psum(partial_solve, "col") * row_live[height][:, None, :]
        interim.append(solved)
        if height + 1 < levels:
            solved_cols = forward_turn(solved)
            for higher in range(height + 1, levels):
                block_slot = pair_index(height, higher, levels)
                update_term = jnp.einsum(
                    "kab,kjb->kja", panels[block_slot], solved_cols, precision=HIGHEST_PRECISION
                )
                update_term = update_term * row_keep[block_slot][:, None, :]
                pending[higher] = pending[higher] + jnp.einsum(
                    "kt,kja->tja", climbs[height, higher], update_term, precision=HIGHEST_PRECISION
                )
    solution = [None] * levels
    for height in reversed(range(levels)):
        if height + 1 < levels:
            carried = jnp.zeros((per_level, rhs_count, col_span), jnp.float32)
            for higher in range(height + 1, levels):
                block_slot = pair_index(height, higher, levels)
                ancestor_part = jnp.einsum(
                    "kt,tja->kja",
                    climbs[height, higher],
                    solution[higher],
                    precision=HIGHEST_PRECISION,
                )
                ancestor_part = ancestor_part * row_keep[block_slot][:, None, :]
                carried = carried + jnp.einsum(
                    "kab,kja->kjb", panels[block_slot], ancestor_part, precision=HIGHEST_PRECISION
                )
            total_carried = lax.psum(carried, "row")
            remaining = interim[height] - backward_turn(total_carried)
        else:
            remaining = interim[height]
        masked = remaining * row_live[height][:, None, :]
        partial_back = jnp.einsum(
            "kab,kja->kjb", diag_inverse[height], masked, precision=HIGHEST_PRECISION
        )
        back_cols = lax.psum(partial_back, "row") * col_live[height][:, None, :]
        solution[height] = backward_turn(back_cols)
    return (jnp.stack(interim), jnp.stack(solution))


def solution(mesh):
    return jax.shard_map(
        per_device,
        mesh=mesh,
        in_specs=(
            P(None, None, None, "row"),
            P(None, None, "row", "col"),
            P(None, None, "row", "col"),
            P(),
            P(),
            P(),
        ),
        out_specs=(P(None, None, None, "row"), P(None, None, None, "row")),
        check_vma=False,
    )
```

profile of v0, /device:TPU:0, one launch (start us, length us, event | category | flops | bytes accessed | tf_op | source)
XLA Modules:
  0.0 1556.6 jit_solution(9475857177889159699)
XLA Ops:
  9.9 19.7 %all-gather.54.cloned.1.call-done = f32[1,2,64,2048]{3,2,1,0:T(8,128)} async-done(((f32[1,2,64,512]{3,2,1,0:T(8,128)}), f32[1,2,64,2048]{3,2,1,0:T(8,128)}) %all-gather.54.cloned.1.call-update) | async-done | bytes 1048592 | tf_op jit(solution)/shard_map/all_gather | solution.py:50
  32.8 71.7 %all-reduce.19.cloned.1.call-done = f32[2,64,512]{2,1,0:T(8,128)} async-done(((f32[2,64,512]{2,1,0:T(8,128)}), f32[2,64,512]{2,1,0:T(8,128)}) %all-reduce.19.cloned.1.call-update) | async-done | bytes 262160 | tf_op jit(solution)/shard_map/psum | solution.py:69
  126.8 71.1 %all-reduce.21.cloned.1.call-done = f32[2,64,512]{2,1,0:T(8,128)} async-done(((f32[2,64,512]{2,1,0:T(8,128)}), f32[2,64,512]{2,1,0:T(8,128)}) %all-reduce.21.cloned.1.call-update) | async-done | bytes 262160 | tf_op jit(solution)/shard_map/psum | solution.py:61
  199.6 16.2 %all-gather.22.cloned.1.call-done = f32[2,64,2048]{2,1,0:T(8,128)} async-done(((f32[2,64,512]{2,1,0:T(8,128)}), f32[2,64,2048]{2,1,0:T(8,128)}) %all-gather.22.cloned.1.call-update) | async-done | bytes 1048592 | tf_op jit(solution)/shard_map/all_gather | solution.py:50
  219.0 71.7 %all-reduce.23.cloned.1.call-done = f32[2,64,512]{2,1,0:T(8,128)} async-done(((f32[2,64,512]{2,1,0:T(8,128)}), f32[2,64,512]{2,1,0:T(8,128)}) %all-reduce.23.cloned.1.call-update) | async-done | bytes 262160 | tf_op jit(solution)/shard_map/psum | solution.py:69
  312.6 71.1 %all-reduce.25.cloned.1.call-done = f32[2,64,512]{2,1,0:T(8,128)} async-done(((f32[2,64,512]{2,1,0:T(8,128)}), f32[2,64,512]{2,1,0:T(8,128)}) %all-reduce.25.cloned.1.call-update) | async-done | bytes 262160 | tf_op jit(solution)/shard_map/psum | solution.py:61
  385.5 16.3 %all-gather.26.cloned.1.call-done = f32[2,64,2048]{2,1,0:T(8,128)} async-done(((f32[2,64,512]{2,1,0:T(8,128)}), f32[2,64,2048]{2,1,0:T(8,128)}) %all-gather.26.cloned.1.call-update) | async-done | bytes 1048592 | tf_op jit(solution)/shard_map/all_gather | solution.py:50
  405.1 71.5 %all-reduce.27.cloned.1.call-done = f32[2,64,512]{2,1,0:T(8,128)} async-done(((f32[2,64,512]{2,1,0:T(8,128)}), f32[2,64,512]{2,1,0:T(8,128)}) %all-reduce.27.cloned.1.call-update) | async-done | bytes 262160 | tf_op jit(solution)/shard_map/psum | solution.py:69
  498.6 71.1 %all-reduce.29.cloned.1.call-done = f32[2,64,512]{2,1,0:T(8,128)} async-done(((f32[2,64,512]{2,1,0:T(8,128)}), f32[2,64,512]{2,1,0:T(8,128)}) %all-reduce.29.cloned.1.call-update) | async-done | bytes 262160 | tf_op jit(solution)/shard_map/psum | solution.py:61
  571.5 16.3 %all-gather.30.cloned.1.call-done = f32[2,64,2048]{2,1,0:T(8,128)} async-done(((f32[2,64,512]{2,1,0:T(8,128)}), f32[2,64,2048]{2,1,0:T(8,128)}) %all-gather.30.cloned.1.call-update) | async-done | bytes 1048592 | tf_op jit(solution)/shard_map/all_gather | solution.py:50
  591.5 71.2 %all-reduce.31.cloned.1.call-done = f32[2,64,512]{2,1,0:T(8,128)} async-done(((f32[2,64,512]{2,1,0:T(8,128)}), f32[2,64,512]{2,1,0:T(8,128)}) %all-reduce.31.cloned.1.call-update) | async-done | bytes 262160 | tf_op jit(solution)/shard_map/psum | solution.py:69
  684.8 71.1 %all-reduce.33.cloned.1.call-done = f32[2,64,512]{2,1,0:T(8,128)} async-done(((f32[2,64,512]{2,1,0:T(8,128)}), f32[2,64,512]{2,1,0:T(8,128)}) %all-reduce.33.cloned.1.call-update) | async-done | bytes 262160 | tf_op jit(solution)/shard_map/psum | solution.py:61
  757.7 16.0 %all-gather.34.cloned.1.call-done = f32[2,64,2048]{2,1,0:T(8,128)} async-done(((f32[2,64,512]{2,1,0:T(8,128)}), f32[2,64,2048]{2,1,0:T(8,128)}) %all-gather.34.cloned.1.call-update) | async-done | bytes 1048592 | tf_op jit(solution)/shard_map/all_gather | solution.py:50
  776.9 71.1 %all-reduce.35.cloned.1.call-done = f32[2,64,512]{2,1,0:T(8,128)} async-done(((f32[2,64,512]{2,1,0:T(8,128)}), f32[2,64,512]{2,1,0:T(8,128)}) %all-reduce.35.cloned.1.call-update) | async-done | bytes 262160 | tf_op jit(solution)/shard_map/psum | solution.py:69
  850.9 31.1 %all-reduce.37.cloned.1.call-done = f32[2,64,256]{2,1,0:T(8,128)} async-done(((f32[2,64,256]{2,1,0:T(8,128)}), f32[2,64,256]{2,1,0:T(8,128)}) %all-reduce.37.cloned.1.call-update) | async-done | bytes 131088 | tf_op jit(solution)/shard_map/psum | solution.py:106
  883.6 39.7 %all-gather.36.cloned.1.call-done = f32[2,64,2048]{2,1,0:T(8,128)} async-done(((f32[2,64,256]{2,1,0:T(8,128)}), f32[2,64,2048]{2,1,0:T(8,128)}) %all-gather.36.cloned.1.call-update) | async-done | bytes 1048592 | tf_op jit(solution)/shard_map/all_gather | solution.py:54
  927.7 30.9 %all-reduce.39.cloned.1.call-done = f32[2,64,256]{2,1,0:T(8,128)} async-done(((f32[2,64,256]{2,1,0:T(8,128)}), f32[2,64,256]{2,1,0:T(8,128)}) %all-reduce.39.cloned.1.call-update) | async-done | bytes 131088 | tf_op jit(solution)/shard_map/psum | solution.py:98
  958.9 41.2 %all-gather.38.cloned.1.call-done = f32[2,64,2048]{2,1,0:T(8,128)} async-done(((f32[2,64,256]{2,1,0:T(8,128)}), f32[2,64,2048]{2,1,0:T(8,128)}) %all-gather.38.cloned.1.call-update) | async-done | bytes 1048592 | tf_op jit(solution)/shard_map/all_gather | solution.py:54
  1002.9 30.9 %all-reduce.41.cloned.1.call-done = f32[2,64,256]{2,1,0:T(8,128)} async-done(((f32[2,64,256]{2,1,0:T(8,128)}), f32[2,64,256]{2,1,0:T(8,128)}) %all-reduce.41.cloned.1.call-update) | async-done | bytes 131088 | tf_op jit(solution)/shard_map/psum | solution.py:106
  1036.6 38.6 %all-gather.40.cloned.1.call-done = f32[2,64,2048]{2,1,0:T(8,128)} async-done(((f32[2,64,256]{2,1,0:T(8,128)}), f32[2,64,2048]{2,1,0:T(8,128)}) %all-gather.40.cloned.1.call-update) | async-done | bytes 1048592 | tf_op jit(solution)/shard_map/all_gather | solution.py:54
  1081.7 30.9 %all-reduce.43.cloned.1.call-done = f32[2,64,256]{2,1,0:T(8,128)} async-done(((f32[2,64,256]{2,1,0:T(8,128)}), f32[2,64,256]{2,1,0:T(8,128)}) %all-reduce.43.cloned.1.call-update) | async-done | bytes 131088 | tf_op jit(solution)/shard_map/psum | solution.py:98
  1112.7 41.2 %all-gather.42.cloned.1.call-done = f32[2,64,2048]{2,1,0:T(8,128)} async-done(((f32[2,64,256]{2,1,0:T(8,128)}), f32[2,64,2048]{2,1,0:T(8,128)}) %all-gather.42.cloned.1.call-update) | async-done | bytes 1048592 | tf_op jit(solution)/shard_map/all_gather | solution.py:54
  1156.8 30.9 %all-reduce.45.cloned.1.call-done = f32[2,64,256]{2,1,0:T(8,128)} async-done(((f32[2,64,256]{2,1,0:T(8,128)}), f32[2,64,256]{2,1,0:T(8,128)}) %all-reduce.45.cloned.1.call-update) | async-done | bytes 131088 | tf_op jit(solution)/shard_map/psum | solution.py:106
  1191.5 37.6 %all-gather.44.cloned.1.call-done = f32[2,64,2048]{2,1,0:T(8,128)} async-done(((f32[2,64,256]{2,1,0:T(8,128)}), f32[2,64,2048]{2,1,0:T(8,128)}) %all-gather.44.cloned.1.call-update) | async-done | bytes 1048592 | tf_op jit(solution)/shard_map/all_gather | solution.py:54
  1237.7 30.9 %all-reduce.47.cloned.1.call-done = f32[2,64,256]{2,1,0:T(8,128)} async-done(((f32[2,64,256]{2,1,0:T(8,128)}), f32[2,64,256]{2,1,0:T(8,128)}) %all-reduce.47.cloned.1.call-update) | async-done | bytes 131088 | tf_op jit(solution)/shard_map/psum | solution.py:98
  1268.7 41.2 %all-gather.46.cloned.1.call-done = f32[2,64,2048]{2,1,0:T(8,128)} async-done(((f32[2,64,256]{2,1,0:T(8,128)}), f32[2,64,2048]{2,1,0:T(8,128)}) %all-gather.46.cloned.1.call-update) | async-done | bytes 1048592 | tf_op jit(solution)/shard_map/all_gather | solution.py:54
  1312.7 30.9 %all-reduce.49.cloned.1.call-done = f32[2,64,256]{2,1,0:T(8,128)} async-done(((f32[2,64,256]{2,1,0:T(8,128)}), f32[2,64,256]{2,1,0:T(8,128)}) %all-reduce.49.cloned.1.call-update) | async-done | bytes 131088 | tf_op jit(solution)/shard_map/psum | solution.py:106
  1348.8 36.3 %all-gather.48.cloned.1.call-done = f32[2,64,2048]{2,1,0:T(8,128)} async-done(((f32[2,64,256]{2,1,0:T(8,128)}), f32[2,64,2048]{2,1,0:T(8,128)}) %all-gather.48.cloned.1.call-update) | async-done | bytes 1048592 | tf_op jit(solution)/shard_map/all_gather | solution.py:54
  1395.6 30.9 %all-reduce.51.cloned.1.call-done = f32[2,64,256]{2,1,0:T(8,128)} async-done(((f32[2,64,256]{2,1,0:T(8,128)}), f32[2,64,256]{2,1,0:T(8,128)}) %all-reduce.51.cloned.1.call-update) | async-done | bytes 131088 | tf_op jit(solution)/shard_map/psum | solution.py:98
  1426.6 41.4 %all-gather.50.cloned.1.call-done = f32[2,64,2048]{2,1,0:T(8,128)} async-done(((f32[2,64,256]{2,1,0:T(8,128)}), f32[2,64,2048]{2,1,0:T(8,128)}) %all-gather.50.cloned.1.call-update) | async-done | bytes 1048592 | tf_op jit(solution)/shard_map/all_gather | solution.py:54
  1470.9 30.9 %all-reduce.53.cloned.1.call-done = f32[2,64,256]{2,1,0:T(8,128)} async-done(((f32[2,64,256]{2,1,0:T(8,128)}), f32[2,64,256]{2,1,0:T(8,128)}) %all-reduce.53.cloned.1.call-update) | async-done | bytes 131088 | tf_op jit(solution)/shard_map/psum | solution.py:106
  1504.1 39.5 %all-gather.52.cloned.1.call-done = f32[2,64,2048]{2,1,0:T(8,128)} async-done(((f32[2,64,256]{2,1,0:T(8,128)}), f32[2,64,2048]{2,1,0:T(8,128)}) %all-gather.52.cloned.1.call-update) | async-done | bytes 1048592 | tf_op jit(solution)/shard_map/all_gather | solution.py:54
  (202 shorter events, 180.2 us)
Async XLA Ops:
  9.0 95.6 %all-reduce.19.cloned.1.call-start = ((), (), s32[]{:S(2)}) async-start(), calls=%async_computation | async-start | bytes 524288 | tf_op jit(solution)/shard_map/psum | solution.py:69
  32.7 89.9 %all-gather.20.cloned.1.call-start = ((), (), s32[]{:S(2)}) async-start(), calls=%async_computation.1 | async-start | bytes 1310720 | tf_op jit(solution)/shard_map/all_gather | solution.py:50
  106.3 91.6 %all-reduce.21.cloned.1.call-start = ((), (), s32[]{:S(2)}) async-start(), calls=%async_computation.2 | async-start | bytes 524288 | tf_op jit(solution)/shard_map/psum | solution.py:61
  126.7 89.1 %all-gather.22.cloned.1.call-start = ((), (), s32[]{:S(2)}) async-start(), calls=%async_computation.3 | async-start | bytes 1310720 | tf_op jit(solution)/shard_map/all_gather | solution.py:50
  199.6 91.0 %all-reduce.23.cloned.1.call-start = ((), (), s32[]{:S(2)}) async-start(), calls=%async_computation.4 | async-start | bytes 524288 | tf_op jit(solution)/shard_map/psum | solution.py:69
  218.9 89.5 %all-gather.24.cloned.1.call-start = ((), (), s32[]{:S(2)}) async-start(), calls=%async_computation.5 | async-start | bytes 1310720 | tf_op jit(solution)/shard_map/all_gather | solution.py:50
  292.4 91.3 %all-reduce.25.cloned.1.call-start = ((), (), s32[]{:S(2)}) async-start(), calls=%async_computation.6 | async-start | bytes 524288 | tf_op jit(solution)/shard_map/psum | solution.py:61
  312.6 89.3 %all-gather.26.cloned.1.call-start = ((), (), s32[]{:S(2)}) async-start(), calls=%async_computation.7 | async-start | bytes 1310720 | tf_op jit(solution)/shard_map/all_gather | solution.py:50
  385.4 91.2 %all-reduce.27.cloned.1.call-start = ((), (), s32[]{:S(2)}) async-start(), calls=%async_computation.8 | async-start | bytes 524288 | tf_op jit(solution)/shard_map/psum | solution.py:69
  404.9 89.5 %all-gather.28.cloned.1.call-start = ((), (), s32[]{:S(2)}) async-start(), calls=%async_computation.9 | async-start | bytes 1310720 | tf_op jit(solution)/shard_map/all_gather | solution.py:50
  478.4 91.4 %all-reduce.29.cloned.1.call-start = ((), (), s32[]{:S(2)}) async-start(), calls=%async_computation.10 | async-start | bytes 524288 | tf_op jit(solution)/shard_map/psum | solution.py:61
  498.6 89.3 %all-gather.30.cloned.1.call-start = ((), (), s32[]{:S(2)}) async-start(), calls=%async_computation.11 | async-start | bytes 1310720 | tf_op jit(solution)/shard_map/all_gather | solution.py:50
  571.5 91.2 %all-reduce.31.cloned.1.call-start = ((), (), s32[]{:S(2)}) async-start(), calls=%async_computation.12 | async-start | bytes 524288 | tf_op jit(solution)/shard_map/psum | solution.py:69
  591.0 89.5 %all-gather.32.cloned.1.call-start = ((), (), s32[]{:S(2)}) async-start(), calls=%async_computation.13 | async-start | bytes 1310720 | tf_op jit(solution)/shard_map/all_gather | solution.py:50
  664.4 91.5 %all-reduce.33.cloned.1.call-start = ((), (), s32[]{:S(2)}) async-start(), calls=%async_computation.14 | async-start | bytes 524288 | tf_op jit(solution)/shard_map/psum | solution.py:61
  684.7 89.0 %all-gather.34.cloned.1.call-start = ((), (), s32[]{:S(2)}) async-start(), calls=%async_computation.15 | async-start | bytes 1310720 | tf_op jit(solution)/shard_map/all_gather | solution.py:50
  757.6 90.4 %all-reduce.35.cloned.1.call-start = ((), (), s32[]{:S(2)}) async-start(), calls=%async_computation.16 | async-start | bytes 524288 | tf_op jit(solution)/shard_map/psum | solution.py:69
  776.8 105.1 %all-reduce.37.cloned.1.call-start = ((), (), s32[]{:S(2)}) async-start(), calls=%async_computation.17 | async-start | bytes 262144 | tf_op jit(solution)/shard_map/psum | solution.py:106
  850.8 72.4 %all-gather.36.cloned.1.call-start = ((), (), s32[]{:S(2)}) async-start(), calls=%async_computation.18 | async-start | bytes 1179648 | tf_op jit(solution)/shard_map/all_gather | solution.py:54
  883.5 75.1 %all-reduce.39.cloned.1.call-start = ((), (), s32[]{:S(2)}) async-start(), calls=%async_computation.19 | async-start | bytes 262144 | tf_op jit(solution)/shard_map/psum | solution.py:98
  927.6 72.4 %all-gather.38.cloned.1.call-start = ((), (), s32[]{:S(2)}) async-start(), calls=%async_computation.20 | async-start | bytes 1179648 | tf_op jit(solution)/shard_map/all_gather | solution.py:54
  958.6 75.2 %all-reduce.41.cloned.1.call-start = ((), (), s32[]{:S(2)}) async-start(), calls=%async_computation.21 | async-start | bytes 262144 | tf_op jit(solution)/shard_map/psum | solution.py:106
  1035.4 77.2 %all-reduce.43.cloned.1.call-start = ((), (), s32[]{:S(2)}) async-start(), calls=%async_computation.23 | async-start | bytes 262144 | tf_op jit(solution)/shard_map/psum | solution.py:98
  1112.6 75.1 %all-reduce.45.cloned.1.call-start = ((), (), s32[]{:S(2)}) async-start(), calls=%async_computation.25 | async-start | bytes 262144 | tf_op jit(solution)/shard_map/psum | solution.py:106
  1156.7 72.4 %all-gather.44.cloned.1.call-start = ((), (), s32[]{:S(2)}) async-start(), calls=%async_computation.26 | async-start | bytes 1179648 | tf_op jit(solution)/shard_map/all_gather | solution.py:54
  1189.3 79.3 %all-reduce.47.cloned.1.call-start = ((), (), s32[]{:S(2)}) async-start(), calls=%async_computation.27 | async-start | bytes 262144 | tf_op jit(solution)/shard_map/psum | solution.py:98
  1268.6 75.0 %all-reduce.49.cloned.1.call-start = ((), (), s32[]{:S(2)}) async-start(), calls=%async_computation.29 | async-start | bytes 262144 | tf_op jit(solution)/shard_map/psum | solution.py:106
  1312.7 72.4 %all-gather.48.cloned.1.call-start = ((), (), s32[]{:S(2)}) async-start(), calls=%async_computation.30 | async-start | bytes 1179648 | tf_op jit(solution)/shard_map/all_gather | solution.py:54
  1345.2 81.3 %all-reduce.51.cloned.1.call-start = ((), (), s32[]{:S(2)}) async-start(), calls=%async_computation.31 | async-start | bytes 262144 | tf_op jit(solution)/shard_map/psum | solution.py:98
  1395.6 72.4 %all-gather.50.cloned.1.call-start = ((), (), s32[]{:S(2)}) async-start(), calls=%async_computation.32 | async-start | bytes 1179648 | tf_op jit(solution)/shard_map/all_gather | solution.py:54
  1426.6 75.2 %all-reduce.53.cloned.1.call-start = ((), (), s32[]{:S(2)}) async-start(), calls=%async_computation.33 | async-start | bytes 262144 | tf_op jit(solution)/shard_map/psum | solution.py:106
  1470.8 72.8 %all-gather.52.cloned.1.call-start = ((), (), s32[]{:S(2)}) async-start(), calls=%async_computation.34 | async-start | bytes 1179648 | tf_op jit(solution)/shard_map/all_gather | solution.py:54
  (12 other events, 1644.0 us)
Sparse Core Ops, SparseCore 0:
  10.1 19.4 all-gather.53
  33.5 71.0 all-reduce.18
  126.8 71.0 all-reduce.20
  199.9 15.8 all-gather.21
  219.6 71.0 all-reduce.22
  292.5 15.8 all-gather.23
  312.7 71.0 all-reduce.24
  405.6 71.0 all-reduce.26
  478.5 15.8 all-gather.27
  498.7 71.0 all-reduce.28
  571.9 15.8 all-gather.29
  591.6 71.0 all-reduce.30
  684.8 71.0 all-reduce.32
  777.0 71.0 all-reduce.34
  850.9 30.9 all-reduce.36
  883.8 39.3 all-gather.35
  927.8 30.7 all-reduce.38
  960.7 39.3 all-gather.37
  1003.0 30.7 all-reduce.40
  1035.7 39.3 all-gather.39
  1081.7 30.7 all-reduce.42
  1114.5 39.3 all-gather.41
  1156.8 30.7 all-reduce.44
  1189.7 39.3 all-gather.43
  1237.7 30.7 all-reduce.46
  1270.5 39.3 all-gather.45
  1312.8 30.7 all-reduce.48
  1345.7 39.3 all-gather.47
  1395.7 30.7 all-reduce.50
  1428.6 39.3 all-gather.49
  1470.9 30.7 all-reduce.52
  1504.2 39.3 all-gather.51
  (4 shorter events, 63.4 us)
where the time goes:
time: 1570 us; the launch traced here: 1560 us
  waiting for transfers between devices  1400 us (89%)
  matrix products  98.3 us (6%)
  other arithmetic  25.7 us (2%)
    psum x5, waiting for transfers between devices, per_device(): solved = lax.psum(partial_solve, 'col') * row_live[height][:, None, :]  357 us
    all_gather x9, waiting for transfers between devices, backward_turn(): full_vector = lax.all_gather(values, 'col', axis=2, tiled=True)  357 us
    psum x4, waiting for transfers between devices, per_device(): summed = lax.psum(pending[height], 'col')  285 us
    psum x5, waiting for transfers between devices, per_device(): back_cols = lax.psum(partial_back, 'row') * col_live[height][:, None, :]  155 us
    psum x4, waiting for transfers between devices, per_device(): total_carried = lax.psum(carried, 'row')  124 us
    all_gather x9, waiting for transfers between devices, forward_turn(): full_vector = lax.all_gather(values, 'row', axis=2, tiled=True)  123 us
  transfers between devices with their start and end apart: 36, of which 36 were waited for; matrix products, arithmetic and copies ran while one was open for 2% of the time, Pallas kernels for 0%

commit v1 on v0

--- a/solution.py
+++ b/solution.py
@@ -58,7 +58,9 @@
     interim = []
     for height in range(levels):
         if height > 0:
-            summed = lax.psum(pending[height], "col")
+            own = pending[height]
+            parts = lax.all_gather(own, "col", axis=0, tiled=False)
+            summed = parts.sum(axis=0)
             residual = right_side[height] - summed
         else:
             residual = right_side[height]

time: 1570 us -> 1480 us (0.943)
  waiting for transfers between devices: 1400 us -> 1310 us
    psum x4 -> x0, waiting for transfers between devices: 285 us -> none  [per_device(): summed = lax.psum(pending[height], 'col')]
    all_gather x0 -> x4, waiting for transfers between devices: none -> 197 us  [per_device(): parts = lax.all_gather(own, 'col', axis=0, tiled=False)]
where the time goes in v1:
time: 1480 us; the launch traced here: 1470 us
  waiting for transfers between devices  1310 us (89%)
  matrix products  98 us (7%)
  other arithmetic  25.9 us (2%)
  local copies, waits for them, and re-layouts  17.1 us (1%)
  between operations  14.8 us (1%)
    all_gather x9, waiting for transfers between devices, backward_turn(): full_vector = lax.all_gather(values, 'col', axis=2, tiled=True)  358 us
    psum x5, waiting for transfers between devices, per_device(): solved = lax.psum(partial_solve, 'col') * row_live[height][:, None, :]  356 us
    all_gather x4, waiting for transfers between devices, per_device(): parts = lax.all_gather(own, 'col', axis=0, tiled=False)  197 us
    psum x5, waiting for transfers between devices, per_device(): back_cols = lax.psum(partial_back, 'row') * col_live[height][:, None, :]  155 us
    psum x4, waiting for transfers between devices, per_device(): total_carried = lax.psum(carried, 'row')  124 us
    all_gather x9, waiting for transfers between devices, forward_turn(): full_vector = lax.all_gather(values, 'row', axis=2, tiled=True)  123 us
  transfers between devices with their start and end apart: 36, of which 36 were waited for; matrix products, arithmetic and copies ran while one was open for 2% of the time, Pallas kernels for 0%

profile of v1, /device:TPU:0, one launch (start us, length us, event | category | flops | bytes accessed | tf_op | source)
XLA Modules:
  0.0 1471.8 jit_solution(5883004477351945266)
XLA Ops:
  9.9 19.7 %all-gather.62.cloned.1.call-done = f32[1,2,64,2048]{3,2,1,0:T(8,128)} async-done(((f32[1,2,64,512]{3,2,1,0:T(8,128)}), f32[1,2,64,2048]{3,2,1,0:T(8,128)}) %all-gather.62.cloned.1.call-update) | async-done | bytes 1048592 | tf_op jit(solution)/shard_map/all_gather | solution.py:50
  32.8 71.7 %all-reduce.15.cloned.1.call-done = f32[2,64,512]{2,1,0:T(8,128)} async-done(((f32[2,64,512]{2,1,0:T(8,128)}), f32[2,64,512]{2,1,0:T(8,128)}) %all-reduce.15.cloned.1.call-update) | async-done | bytes 262160 | tf_op jit(solution)/shard_map/psum | solution.py:71
  126.6 49.2 %all-gather.64.cloned.1.call-done = f32[16,64,512]{2,1,0:T(8,128)} async-done(((f32[2,64,512]{2,1,0:T(8,128)}), f32[16,64,512]{2,1,0:T(8,128)}) %all-gather.64.cloned.1.call-update) | async-done | bytes 2097168 | tf_op jit(solution)/shard_map/all_gather | solution.py:62
  178.4 15.3 %all-gather.30.cloned.1.call-done = f32[2,64,2048]{2,1,0:T(8,128)} async-done(((f32[2,64,512]{2,1,0:T(8,128)}), f32[2,64,2048]{2,1,0:T(8,128)}) %all-gather.30.cloned.1.call-update) | async-done | bytes 1048592 | tf_op jit(solution)/shard_map/all_gather | solution.py:50
  197.0 71.6 %all-reduce.17.cloned.1.call-done = f32[2,64,512]{2,1,0:T(8,128)} async-done(((f32[2,64,512]{2,1,0:T(8,128)}), f32[2,64,512]{2,1,0:T(8,128)}) %all-reduce.17.cloned.1.call-update) | async-done | bytes 262160 | tf_op jit(solution)/shard_map/psum | solution.py:71
  292.0 49.2 %all-gather.66.cloned.1.call-done = f32[16,64,512]{2,1,0:T(8,128)} async-done(((f32[2,64,512]{2,1,0:T(8,128)}), f32[16,64,512]{2,1,0:T(8,128)}) %all-gather.66.cloned.1.call-update) | async-done | bytes 2097168 | tf_op jit(solution)/shard_map/all_gather | solution.py:62
  343.8 15.3 %all-gather.34.cloned.1.call-done = f32[2,64,2048]{2,1,0:T(8,128)} async-done(((f32[2,64,512]{2,1,0:T(8,128)}), f32[2,64,2048]{2,1,0:T(8,128)}) %all-gather.34.cloned.1.call-update) | async-done | bytes 1048592 | tf_op jit(solution)/shard_map/all_gather | solution.py:50
  362.4 71.0 %all-reduce.19.cloned.1.call-done = f32[2,64,512]{2,1,0:T(8,128)} async-done(((f32[2,64,512]{2,1,0:T(8,128)}), f32[2,64,512]{2,1,0:T(8,128)}) %all-reduce.19.cloned.1.call-update) | async-done | bytes 262160 | tf_op jit(solution)/shard_map/psum | solution.py:71
  456.6 49.2 %all-gather.68.cloned.1.call-done = f32[16,64,512]{2,1,0:T(8,128)} async-done(((f32[2,64,512]{2,1,0:T(8,128)}), f32[16,64,512]{2,1,0:T(8,128)}) %all-gather.68.cloned.1.call-update) | async-done | bytes 2097168 | tf_op jit(solution)/shard_map/all_gather | solution.py:62
  508.5 15.3 %all-gather.38.cloned.1.call-done = f32[2,64,2048]{2,1,0:T(8,128)} async-done(((f32[2,64,512]{2,1,0:T(8,128)}), f32[2,64,2048]{2,1,0:T(8,128)}) %all-gather.38.cloned.1.call-update) | async-done | bytes 1048592 | tf_op jit(solution)/shard_map/all_gather | solution.py:50
  527.2 70.9 %all-reduce.21.cloned.1.call-done = f32[2,64,512]{2,1,0:T(8,128)} async-done(((f32[2,64,512]{2,1,0:T(8,128)}), f32[2,64,512]{2,1,0:T(8,128)}) %all-reduce.21.cloned.1.call-update) | async-done | bytes 262160 | tf_op jit(solution)/shard_map/psum | solution.py:71
  621.3 49.2 %all-gather.70.cloned.1.call-done = f32[16,64,512]{2,1,0:T(8,128)} async-done(((f32[2,64,512]{2,1,0:T(8,128)}), f32[16,64,512]{2,1,0:T(8,128)}) %all-gather.70.cloned.1.call-update) | async-done | bytes 2097168 | tf_op jit(solution)/shard_map/all_gather | solution.py:62
  673.1 15.3 %all-gather.42.cloned.1.call-done = f32[2,64,2048]{2,1,0:T(8,128)} async-done(((f32[2,64,512]{2,1,0:T(8,128)}), f32[2,64,2048]{2,1,0:T(8,128)}) %all-gather.42.cloned.1.call-update) | async-done | bytes 1048592 | tf_op jit(solution)/shard_map/all_gather | solution.py:50
  691.6 71.1 %all-reduce.23.cloned.1.call-done = f32[2,64,512]{2,1,0:T(8,128)} async-done(((f32[2,64,512]{2,1,0:T(8,128)}), f32[2,64,512]{2,1,0:T(8,128)}) %all-reduce.23.cloned.1.call-update) | async-done | bytes 262160 | tf_op jit(solution)/shard_map/psum | solution.py:71
  765.5 31.1 %all-reduce.25.cloned.1.call-done = f32[2,64,256]{2,1,0:T(8,128)} async-done(((f32[2,64,256]{2,1,0:T(8,128)}), f32[2,64,256]{2,1,0:T(8,128)}) %all-reduce.25.cloned.1.call-update) | async-done | bytes 131088 | tf_op jit(solution)/shard_map/psum | solution.py:108
  798.2 39.7 %all-gather.44.cloned.1.call-done = f32[2,64,2048]{2,1,0:T(8,128)} async-done(((f32[2,64,256]{2,1,0:T(8,128)}), f32[2,64,2048]{2,1,0:T(8,128)}) %all-gather.44.cloned.1.call-update) | async-done | bytes 1048592 | tf_op jit(solution)/shard_map/all_gather | solution.py:54
  842.4 30.9 %all-reduce.27.cloned.1.call-done = f32[2,64,256]{2,1,0:T(8,128)} async-done(((f32[2,64,256]{2,1,0:T(8,128)}), f32[2,64,256]{2,1,0:T(8,128)}) %all-reduce.27.cloned.1.call-update) | async-done | bytes 131088 | tf_op jit(solution)/shard_map/psum | solution.py:100
  873.8 41.0 %all-gather.46.cloned.1.call-done = f32[2,64,2048]{2,1,0:T(8,128)} async-done(((f32[2,64,256]{2,1,0:T(8,128)}), f32[2,64,2048]{2,1,0:T(8,128)}) %all-gather.46.cloned.1.call-update) | async-done | bytes 1048592 | tf_op jit(solution)/shard_map/all_gather | solution.py:54
  917.6 30.9 %all-reduce.29.cloned.1.call-done = f32[2,64,256]{2,1,0:T(8,128)} async-done(((f32[2,64,256]{2,1,0:T(8,128)}), f32[2,64,256]{2,1,0:T(8,128)}) %all-reduce.29.cloned.1.call-update) | async-done | bytes 131088 | tf_op jit(solution)/shard_map/psum | solution.py:108
  951.3 38.6 %all-gather.48.cloned.1.call-done = f32[2,64,2048]{2,1,0:T(8,128)} async-done(((f32[2,64,256]{2,1,0:T(8,128)}), f32[2,64,2048]{2,1,0:T(8,128)}) %all-gather.48.cloned.1.call-update) | async-done | bytes 1048592 | tf_op jit(solution)/shard_map/all_gather | solution.py:54
  996.5 30.9 %all-reduce.31.cloned.1.call-done = f32[2,64,256]{2,1,0:T(8,128)} async-done(((f32[2,64,256]{2,1,0:T(8,128)}), f32[2,64,256]{2,1,0:T(8,128)}) %all-reduce.31.cloned.1.call-update) | async-done | bytes 131088 | tf_op jit(solution)/shard_map/psum | solution.py:100
  1027.5 41.2 %all-gather.50.cloned.1.call-done = f32[2,64,2048]{2,1,0:T(8,128)} async-done(((f32[2,64,256]{2,1,0:T(8,128)}), f32[2,64,2048]{2,1,0:T(8,128)}) %all-gather.50.cloned.1.call-update) | async-done | bytes 1048592 | tf_op jit(solution)/shard_map/all_gather | solution.py:54
  1071.5 30.9 %all-reduce.33.cloned.1.call-done = f32[2,64,256]{2,1,0:T(8,128)} async-done(((f32[2,64,256]{2,1,0:T(8,128)}), f32[2,64,256]{2,1,0:T(8,128)}) %all-reduce.33.cloned.1.call-update) | async-done | bytes 131088 | tf_op jit(solution)/shard_map/psum | solution.py:108
  1106.3 37.7 %all-gather.52.cloned.1.call-done = f32[2,64,2048]{2,1,0:T(8,128)} async-done(((f32[2,64,256]{2,1,0:T(8,128)}), f32[2,64,2048]{2,1,0:T(8,128)}) %all-gather.52.cloned.1.call-update) | async-done | bytes 1048592 | tf_op jit(solution)/shard_map/all_gather | solution.py:54
  1152.5 30.9 %all-reduce.35.cloned.1.call-done = f32[2,64,256]{2,1,0:T(8,128)} async-done(((f32[2,64,256]{2,1,0:T(8,128)}), f32[2,64,256]{2,1,0:T(8,128)}) %all-reduce.35.cloned.1.call-update) | async-done | bytes 131088 | tf_op jit(solution)/shard_map/psum | solution.py:100
  1183.5 41.2 %all-gather.54.cloned.1.call-done = f32[2,64,2048]{2,1,0:T(8,128)} async-done(((f32[2,64,256]{2,1,0:T(8,128)}), f32[2,64,2048]{2,1,0:T(8,128)}) %all-gather.54.cloned.1.call-update) | async-done | bytes 1048592 | tf_op jit(solution)/shard_map/all_gather | solution.py:54
  1227.5 30.9 %all-reduce.37.cloned.1.call-done = f32[2,64,256]{2,1,0:T(8,128)} async-done(((f32[2,64,256]{2,1,0:T(8,128)}), f32[2,64,256]{2,1,0:T(8,128)}) %all-reduce.37.cloned.1.call-update) | async-done | bytes 131088 | tf_op jit(solution)/shard_map/psum | solution.py:108
  1263.5 37.0 %all-gather.56.cloned.1.call-done = f32[2,64,2048]{2,1,0:T(8,128)} async-done(((f32[2,64,256]{2,1,0:T(8,128)}), f32[2,64,2048]{2,1,0:T(8,128)}) %all-gather.56.cloned.1.call-update) | async-done | bytes 1048592 | tf_op jit(solution)/shard_map/all_gather | solution.py:54
  1311.1 30.9 %all-reduce.39.cloned.1.call-done = f32[2,64,256]{2,1,0:T(8,128)} async-done(((f32[2,64,256]{2,1,0:T(8,128)}), f32[2,64,256]{2,1,0:T(8,128)}) %all-reduce.39.cloned.1.call-update) | async-done | bytes 131088 | tf_op jit(solution)/shard_map/psum | solution.py:100
  1342.0 41.4 %all-gather.58.cloned.1.call-done = f32[2,64,2048]{2,1,0:T(8,128)} async-done(((f32[2,64,256]{2,1,0:T(8,128)}), f32[2,64,2048]{2,1,0:T(8,128)}) %all-gather.58.cloned.1.call-update) | async-done | bytes 1048592 | tf_op jit(solution)/shard_map/all_gather | solution.py:54
  1386.3 30.9 %all-reduce.41.cloned.1.call-done = f32[2,64,256]{2,1,0:T(8,128)} async-done(((f32[2,64,256]{2,1,0:T(8,128)}), f32[2,64,256]{2,1,0:T(8,128)}) %all-reduce.41.cloned.1.call-update) | async-done | bytes 131088 | tf_op jit(solution)/shard_map/psum | solution.py:108
  1418.8 40.2 %all-gather.60.cloned.1.call-done = f32[2,64,2048]{2,1,0:T(8,128)} async-done(((f32[2,64,256]{2,1,0:T(8,128)}), f32[2,64,2048]{2,1,0:T(8,128)}) %all-gather.60.cloned.1.call-update) | async-done | bytes 1048592 | tf_op jit(solution)/shard_map/all_gather | solution.py:54
  (208 shorter events, 186.4 us)
Async XLA Ops:
  9.0 95.6 %all-reduce.15.cloned.1.call-start = ((), (), s32[]{:S(2)}) async-start(), calls=%async_computation | async-start | bytes 524288 | tf_op jit(solution)/shard_map/psum | solution.py:71
  32.7 89.9 %all-gather.28.cloned.1.call-start = ((), (), s32[]{:S(2)}) async-start(), calls=%async_computation.1 | async-start | bytes 1310720 | tf_op jit(solution)/shard_map/all_gather | solution.py:50
  106.3 69.5 %all-gather.64.cloned.1.call-start = ((), (), s32[]{:S(2)}) async-start(), calls=%async_computation.32 | async-start | bytes 2359296 | tf_op jit(solution)/shard_map/all_gather | solution.py:62
  178.4 90.2 %all-reduce.17.cloned.1.call-start = ((), (), s32[]{:S(2)}) async-start(), calls=%async_computation.3 | async-start | bytes 524288 | tf_op jit(solution)/shard_map/psum | solution.py:71
  196.9 89.8 %all-gather.32.cloned.1.call-start = ((), (), s32[]{:S(2)}) async-start(), calls=%async_computation.4 | async-start | bytes 1310720 | tf_op jit(solution)/shard_map/all_gather | solution.py:50
  270.4 70.8 %all-gather.66.cloned.1.call-start = ((), (), s32[]{:S(2)}) async-start(), calls=%async_computation.33 | async-start | bytes 2359296 | tf_op jit(solution)/shard_map/all_gather | solution.py:62
  292.0 67.2 %all-gather.34.cloned.1.call-start = ((), (), s32[]{:S(2)}) async-start(), calls=%async_computation.5 | async-start | bytes 1310720 | tf_op jit(solution)/shard_map/all_gather | solution.py:50
  343.8 89.7 %all-reduce.19.cloned.1.call-start = ((), (), s32[]{:S(2)}) async-start(), calls=%async_computation.6 | async-start | bytes 524288 | tf_op jit(solution)/shard_map/psum | solution.py:71
  362.3 89.0 %all-gather.36.cloned.1.call-start = ((), (), s32[]{:S(2)}) async-start(), calls=%async_computation.7 | async-start | bytes 1310720 | tf_op jit(solution)/shard_map/all_gather | solution.py:50
  435.2 70.6 %all-gather.68.cloned.1.call-start = ((), (), s32[]{:S(2)}) async-start(), calls=%async_computation.34 | async-start | bytes 2359296 | tf_op jit(solution)/shard_map/all_gather | solution.py:62
  508.4 89.7 %all-reduce.21.cloned.1.call-start = ((), (), s32[]{:S(2)}) async-start(), calls=%async_computation.9 | async-start | bytes 524288 | tf_op jit(solution)/shard_map/psum | solution.py:71
  527.0 88.9 %all-gather.40.cloned.1.call-start = ((), (), s32[]{:S(2)}) async-start(), calls=%async_computation.10 | async-start | bytes 1310720 | tf_op jit(solution)/shard_map/all_gather | solution.py:50
  599.8 70.6 %all-gather.70.cloned.1.call-start = ((), (), s32[]{:S(2)}) async-start(), calls=%async_computation.35 | async-start | bytes 2359296 | tf_op jit(solution)/shard_map/all_gather | solution.py:62
  673.0 89.7 %all-reduce.23.cloned.1.call-start = ((), (), s32[]{:S(2)}) async-start(), calls=%async_computation.12 | async-start | bytes 524288 | tf_op jit(solution)/shard_map/psum | solution.py:71
  691.5 105.1 %all-reduce.25.cloned.1.call-start = ((), (), s32[]{:S(2)}) async-start(), calls=%async_computation.13 | async-start | bytes 262144 | tf_op jit(solution)/shard_map/psum | solution.py:108
  765.5 72.4 %all-gather.44.cloned.1.call-start = ((), (), s32[]{:S(2)}) async-start(), calls=%async_computation.14 | async-start | bytes 1179648 | tf_op jit(solution)/shard_map/all_gather | solution.py:54
  798.2 75.2 %all-reduce.27.cloned.1.call-start = ((), (), s32[]{:S(2)}) async-start(), calls=%async_computation.15 | async-start | bytes 262144 | tf_op jit(solution)/shard_map/psum | solution.py:100
  842.4 72.4 %all-gather.46.cloned.1.call-start = ((), (), s32[]{:S(2)}) async-start(), calls=%async_computation.16 | async-start | bytes 1179648 | tf_op jit(solution)/shard_map/all_gather | solution.py:54
  873.4 75.2 %all-reduce.29.cloned.1.call-start = ((), (), s32[]{:S(2)}) async-start(), calls=%async_computation.17 | async-start | bytes 262144 | tf_op jit(solution)/shard_map/psum | solution.py:108
  917.6 72.3 %all-gather.48.cloned.1.call-start = ((), (), s32[]{:S(2)}) async-start(), calls=%async_computation.18 | async-start | bytes 1179648 | tf_op jit(solution)/shard_map/all_gather | solution.py:54
  950.1 77.2 %all-reduce.31.cloned.1.call-start = ((), (), s32[]{:S(2)}) async-start(), calls=%async_computation.19 | async-start | bytes 262144 | tf_op jit(solution)/shard_map/psum | solution.py:100
  996.4 72.3 %all-gather.50.cloned.1.call-start = ((), (), s32[]{:S(2)}) async-start(), calls=%async_computation.20 | async-start | bytes 1179648 | tf_op jit(solution)/shard_map/all_gather | solution.py:54
  1027.4 75.0 %all-reduce.33.cloned.1.call-start = ((), (), s32[]{:S(2)}) async-start(), calls=%async_computation.21 | async-start | bytes 262144 | tf_op jit(solution)/shard_map/psum | solution.py:108
  1071.5 72.4 %all-gather.52.cloned.1.call-start = ((), (), s32[]{:S(2)}) async-start(), calls=%async_computation.22 | async-start | bytes 1179648 | tf_op jit(solution)/shard_map/all_gather | solution.py:54
  1104.0 79.3 %all-reduce.35.cloned.1.call-start = ((), (), s32[]{:S(2)}) async-start(), calls=%async_computation.23 | async-start | bytes 262144 | tf_op jit(solution)/shard_map/psum | solution.py:100
  1152.4 72.3 %all-gather.54.cloned.1.call-start = ((), (), s32[]{:S(2)}) async-start(), calls=%async_computation.24 | async-start | bytes 1179648 | tf_op jit(solution)/shard_map/all_gather | solution.py:54
  1183.4 75.0 %all-reduce.37.cloned.1.call-start = ((), (), s32[]{:S(2)}) async-start(), calls=%async_computation.25 | async-start | bytes 262144 | tf_op jit(solution)/shard_map/psum | solution.py:108
  1227.5 73.0 %all-gather.56.cloned.1.call-start = ((), (), s32[]{:S(2)}) async-start(), calls=%async_computation.26 | async-start | bytes 1179648 | tf_op jit(solution)/shard_map/all_gather | solution.py:54
  1260.0 81.9 %all-reduce.39.cloned.1.call-start = ((), (), s32[]{:S(2)}) async-start(), calls=%async_computation.27 | async-start | bytes 262144 | tf_op jit(solution)/shard_map/psum | solution.py:100
  1311.0 72.4 %all-gather.58.cloned.1.call-start = ((), (), s32[]{:S(2)}) async-start(), calls=%async_computation.28 | async-start | bytes 1179648 | tf_op jit(solution)/shard_map/all_gather | solution.py:54
  1342.0 75.2 %all-reduce.41.cloned.1.call-start = ((), (), s32[]{:S(2)}) async-start(), calls=%async_computation.29 | async-start | bytes 262144 | tf_op jit(solution)/shard_map/psum | solution.py:108
  1386.2 72.9 %all-gather.60.cloned.1.call-start = ((), (), s32[]{:S(2)}) async-start(), calls=%async_computation.30 | async-start | bytes 1179648 | tf_op jit(solution)/shard_map/all_gather | solution.py:54
  (12 other events, 1625.8 us)
Sparse Core Ops, SparseCore 0:
  10.1 19.4 all-gather.61
  33.5 71.0 all-reduce.14
  106.7 15.8 all-gather.27
  126.7 49.0 all-gather.63
  197.6 70.9 all-reduce.16
  270.7 15.8 all-gather.31
  292.1 49.0 all-gather.65
  362.4 70.9 all-reduce.18
  435.4 15.8 all-gather.35
  456.7 49.0 all-gather.67
  527.1 70.9 all-reduce.20
  600.0 15.8 all-gather.39
  621.3 49.0 all-gather.69
  691.6 70.9 all-reduce.22
  765.6 30.9 all-reduce.24
  798.5 39.3 all-gather.43
  842.5 30.7 all-reduce.26
  875.4 39.3 all-gather.45
  917.7 30.7 all-reduce.28
  950.5 39.3 all-gather.47
  996.5 30.7 all-reduce.30
  1029.3 39.3 all-gather.49
  1071.6 30.7 all-reduce.32
  1104.5 39.3 all-gather.51
  1152.5 30.7 all-reduce.34
  1185.3 39.3 all-gather.53
  1227.6 30.7 all-reduce.36
  1261.1 39.3 all-gather.55
  1311.1 30.7 all-reduce.38
  1344.0 39.3 all-gather.57
  1386.4 30.7 all-reduce.40
  1419.7 39.3 all-gather.59
  (4 shorter events, 60.7 us)
